TPU v7x, 32 devices: a whole 2x2x4 slice. The times are simulated.
32 devices in a mesh: groups: 2 (over x), aux: 16 (over z, y, core).
Axes of the slice: x: 2, y: 2, z: 4, core: 2. Of those that a mesh axis runs over, the one named last changes fastest.
Arguments:
- slabs: bfloat16 [8000, 23040], P(('groups', 'aux')), parts along dimension 0, may hold values from -2 to 2
- rdm: bfloat16 [1800, 900], P('groups'), parts along dimension 0, as said below
- orbital_energy: float32 [1536], P('groups'), parts along dimension 0, may hold values from 0.5 to 3
- pair_blocks: int32 [32, 2], P('groups'), parts along dimension 0, may hold values from 0 to 15, as said below
Outputs:
- pair_energy: float32 [1536, 48], P(('groups', 'aux')), parts along dimension 0
- window_energy: float32 [2], P('groups'), parts along dimension 0
There are 2 independent parts, one for each index of `groups`. A program takes and returns all parts, laid end to end along the dimension named above; each array names one. Nothing has to cross between parts.
Inputs may be any that keep to these rules, and one draw needn't show every extreme that they name: `pair_blocks`: each row (p, q) has p <= q, and no two rows are equal. `rdm`: symmetric.
All inputs are finite; a program needn't handle non-finite values.
Results may differ from a plain program's by a relative error of at most 0.002.
Values may be sent and summed in bfloat16 or wider, within the bound.
A program may use at most 128 MiB of HBM per device.

v0:
```python
import jax
import jax.numpy as jnp
from jax import lax
from jax.sharding import PartitionSpec as P

NACT = 30
VBLK = 48
NBLK = 16


def per_device(slabs, rdm, orbital_energy, pair_blocks):
    local_rows = slabs.shape[0]
    width = VBLK * NACT
    blocked = slabs.reshape(local_rows, NBLK, width)
    position = lax.axis_index("aux")
    row_block = pair_blocks[position, 0]
    col_block = pair_blocks[position, 1]
    outgoing_rows = jnp.take(blocked, pair_blocks[:, 0], axis=1)
    arrived_rows = lax.all_to_all(outgoing_rows, "aux", split_axis=1, concat_axis=0, tiled=True)
    row_part = arrived_rows.reshape(-1, width)
    outgoing_cols = jnp.take(blocked, pair_blocks[:, 1], axis=1)
    columns = lax.all_to_all(outgoing_cols, "aux", split_axis=1, concat_axis=0, tiled=True)
    flattened = columns.reshape(columns.shape[0], -1)
    products = lax.dot_general(
        row_part, flattened, (((0,), (0,)), ((), ())), preferred_element_type=jnp.float32
    )
    integrals = products.astype(jnp.bfloat16)
    reordered = (
        integrals.reshape(VBLK, NACT, VBLK, NACT)
        .transpose(0, 2, 1, 3)
        .reshape(VBLK * VBLK, NACT * NACT)
    )
    contracted = jnp.dot(reordered, rdm, preferred_element_type=jnp.float32)
    paired = jnp.sum(contracted * reordered.astype(jnp.float32), axis=1).reshape(VBLK, VBLK)
    energy_rows = lax.dynamic_slice_in_dim(orbital_energy, row_block * VBLK, VBLK)
    energy_cols = lax.dynamic_slice_in_dim(orbital_energy, col_block * VBLK, VBLK)
    energy = -paired / (energy_rows[:, None] + energy_cols[None, :])
    weight = jnp.where(row_block == col_block, jnp.float32(1.0), jnp.float32(2.0))
    total = lax.psum(weight * jnp.sum(energy), "aux")
    mean_energy = total / (VBLK * VBLK * lax.axis_size("aux"))
    return (energy, mean_energy.reshape(1))


def solution(mesh):
    return jax.shard_map(
        per_device,
        mesh=mesh,
        in_specs=(P(("groups", "aux"), None), P("groups", None), P("groups"), P("groups", None)),
        out_specs=(P(("groups", "aux"), None), P("groups")),
        check_vma=False,
    )
```

profile of v0, /device:TPU:0, one launch (start us, length us, event | category | flops | bytes accessed | tf_op | source)
XLA Modules:
  0.0 696.6 jit_solution(6282862908043864773)
XLA Ops:
  0.6 0.0 copy-start
  0.6 0.0 copy-start.1
  0.7 16.4 %copy.7 = bf16[250,23040]{0,1:T(8,128)(2,1)} copy(bf16[250,23040]{1,0:T(8,128)(2,1)} %param.6) | data formatting | bytes 23040000 | tf_op args[0]
  17.1 0.0 copy-done.1
  17.1 10.5 %gather_fusion.1 = bf16[16,250,1440]{1,2,0:T(8,128)(2,1)} fusion(bf16[250,16,1440]{0,2,1:T(8,128)(2,1)} %bitcast.42, s32[1024]{0:T(1024)S(1)} %pad_clamp_fusion), kind=kCustom, calls=%fused_computation.1.clone | custom fusion | bytes 23040064 | tf_op jit(solution)/shard_map/jit(_take)/gather | solution.py:21
  27.6 10.3 %select_bitcast_fusion = bf16[250,16,1440]{0,2,1:T(8,128)(2,1)} fusion(bf16[16,250,1440]{1,2,0:T(8,128)(2,1)} %gather_fusion.1, pred[16]{0:T(512)(128)(4,1)S(1)} %get-tuple-element.13), kind=kLoop, calls=%fused_computation.5 | loop fusion | flops 5760000 | bytes 23040016 | tf_op jit(solution)/shard_map/jit(_take)/select_n | solution.py:21
  37.9 7.5 %all-to-all-start.1 = ((bf16[250,16,1440]{0,2,1:T(8,128)(2,1)}), bf16[250,16,1440]{0,2,1:T(8,128)(2,1)}, u32[]{:S(2)}, u32[]{:S(2)}) async-start(bf16[250,16,1440]{0,2,1:T(8,128)(2,1)} %select_bitcast_fusion), calls=%async_computation.1 | async-start | bytes 23592960 | tf_op jit(solution)/shard_map/all_to_all | solution.py:22
  45.4 10.4 %gather_fusion = bf16[16,250,1440]{1,2,0:T(8,128)(2,1)} fusion(bf16[250,16,1440]{0,2,1:T(8,128)(2,1)} %bitcast.43, s32[1024]{0:T(1024)S(1)} %pad_clamp_fusion.1), kind=kCustom, calls=%fused_computation.clone | custom fusion | bytes 23040064 | tf_op jit(solution)/shard_map/jit(_take)/gather | solution.py:18
  55.8 10.3 %select_bitcast_fusion.1 = bf16[250,16,1440]{0,2,1:T(8,128)(2,1)} fusion(bf16[16,250,1440]{1,2,0:T(8,128)(2,1)} %gather_fusion, pred[16]{0:T(512)(128)(4,1)S(1)} %get-tuple-element.5), kind=kLoop, calls=%fused_computation.6 | loop fusion | flops 5760000 | bytes 23040016 | tf_op jit(solution)/shard_map/jit(_take)/select_n | solution.py:18
  66.1 189.2 %all-to-all-done.1 = bf16[250,16,1440]{0,2,1:T(8,128)(2,1)} async-done(((bf16[250,16,1440]{0,2,1:T(8,128)(2,1)}), bf16[250,16,1440]{0,2,1:T(8,128)(2,1)}, u32[]{:S(2)}, u32[]{:S(2)}) %all-to-all-start.1) | async-done | bytes 11520032 | tf_op jit(solution)/shard_map/all_to_all | solution.py:22
  255.3 50.2 %all-to-all-start = ((bf16[250,16,1440]{0,2,1:T(8,128)(2,1)}), bf16[250,16,1440]{0,2,1:T(8,128)(2,1)}, u32[]{:S(2)}, u32[]{:S(2)}) async-start(bf16[250,16,1440]{0,2,1:T(8,128)(2,1)} %select_bitcast_fusion.1), calls=%async_computation | async-start | bytes 23592960 | tf_op jit(solution)/shard_map/all_to_all | solution.py:19
  305.5 0.6 constant_dynamic-slice_fusion.1
  308.7 0.8 fusion.8
  309.6 205.9 %all-to-all-done = bf16[250,16,1440]{0,2,1:T(8,128)(2,1)} async-done(((bf16[250,16,1440]{0,2,1:T(8,128)(2,1)}), bf16[250,16,1440]{0,2,1:T(8,128)(2,1)}, u32[]{:S(2)}, u32[]{:S(2)}) %all-to-all-start) | async-done | bytes 11520032 | tf_op jit(solution)/shard_map/all_to_all | solution.py:19
  515.4 25.4 %bitcast_convert_fusion = bf16[1440,1440]{1,0:T(8,128)(2,1)} fusion(bf16[250,16,1440]{0,2,1:T(8,128)(2,1)} %all-to-all-done.1, bf16[250,16,1440]{0,2,1:T(8,128)(2,1)} %all-to-all-done), kind=kOutput, calls=%fused_computation.7 | convolution fusion | flops 16590873600 | bytes 27187200 | tf_op jit(solution)/shard_map/dot_general | solution.py:24
  540.8 26.9 %reshape.52 = bf16[48,30,48,30]{3,2,1,0:T(8,128)(2,1)} reshape(bf16[1440,1440]{1,0:T(8,128)(2,1)} %bitcast_convert_fusion) | data formatting | bytes 8294400 | tf_op jit(solution)/shard_map/reshape | solution.py:29
  567.7 21.3 %copy.8 = bf16[48,48,30,30]{1,0,3,2:T(8,128)(2,1)} copy(bf16[48,48,30,30]{3,1,2,0:T(8,128)(2,1)} %bitcast.44) | data formatting | bytes 8294400 | tf_op jit(solution)/shard_map/transpose | solution.py:30
  589.0 16.1 %reshape.53 = bf16[2304,900]{0,1:T(8,128)(2,1)} reshape(bf16[48,48,30,30]{1,0,3,2:T(8,128)(2,1)} %copy.8) | data formatting | bytes 8294400 | tf_op jit(solution)/shard_map/reshape | solution.py:31
  605.1 0.0 copy-done
  605.1 8.9 %multiply_reduce_fusion = f32[2304]{0:T(1024)S(1)} fusion(bf16[2304,900]{0,1:T(8,128)(2,1)} %reshape.53, bf16[900,900]{1,0:T(8,128)(2,1)S(1)} %copy-done), kind=kOutput, calls=%fused_computation.8 | convolution fusion | flops 3738698496 | bytes 5776416 | tf_op jit(solution)/shard_map/dot_general | solution.py:33
  614.0 0.1 neg.11
  614.0 1.3 fusion.7
  616.0 78.8 %psum.7 = f32[]{:T(128)} all-reduce(f32[]{:T(128)S(6)} %mul.23), channel_id=1, replica_groups=mesh['groups'=2,'aux'=16] {'aux'}, use_global_device_ids=true, to_apply=%region_2.4 | all-reduce | flops 1 | bytes 8 | tf_op jit(solution)/shard_map/psum | solution.py:39
  (4 shorter events, 0.0 us)
Async XLA Ops:
  0.6 604.5 %copy-start = (bf16[900,900]{1,0:T(8,128)(2,1)S(1)}, bf16[900,900]{1,0:T(8,128)(2,1)}, u32[]{:S(2)}) copy-start(bf16[900,900]{1,0:T(8,128)(2,1)} %param.7) | copy-start | bytes 4860004
  0.6 16.4 %copy-start.1 = (s32[16,2]{0,1:T(2,128)S(1)}, s32[16,2]{0,1:T(2,128)}, u32[]{:S(2)}) copy-start(s32[16,2]{0,1:T(2,128)} %param.9) | copy-start | bytes 388
  37.9 217.4 %all-to-all-start.1 = ((bf16[250,16,1440]{0,2,1:T(8,128)(2,1)}), bf16[250,16,1440]{0,2,1:T(8,128)(2,1)}, u32[]{:S(2)}, u32[]{:S(2)}) async-start(bf16[250,16,1440]{0,2,1:T(8,128)(2,1)} %select_bitcast_fusion), calls=%async_computation.1 | async-start | bytes 23592960 | tf_op jit(solution)/shard_map/all_to_all | solution.py:22
  255.3 260.2 %all-to-all-start = ((bf16[250,16,1440]{0,2,1:T(8,128)(2,1)}), bf16[250,16,1440]{0,2,1:T(8,128)(2,1)}, u32[]{:S(2)}, u32[]{:S(2)}) async-start(bf16[250,16,1440]{0,2,1:T(8,128)(2,1)} %select_bitcast_fusion.1), calls=%async_computation | async-start | bytes 23592960 | tf_op jit(solution)/shard_map/all_to_all | solution.py:19
where the time goes:
time: 699 us; the launch traced here: 697 us
  waiting for transfers between devices  395 us (57%)
  local copies, waits for them, and re-layouts  103 us (15%)
  blocking collectives  78.8 us (11%)
  starting transfers between devices  57.7 us (8%)
  matrix products  34.2 us (5%)
  other arithmetic  21.9 us (3%)
    all_to_all x1, waiting for transfers between devices, per_device(): lax.all_to_all(outgoing_rows, 'aux', split_axis=1, concat_axis=0, tiled=T...  206 us
    all_to_all x1, waiting for transfers between devices, per_device(): lax.all_to_all(outgoing_cols, 'aux', split_axis=1, concat_axis=0, tiled=T...  189 us
    psum x1, blocking collectives, per_device(): total = lax.psum(weight * jnp.sum(energy), 'aux')  78.8 us
    all_to_all x1, starting transfers between devices, per_device(): lax.all_to_all(outgoing_rows, 'aux', split_axis=1, concat_axis=0, tiled=T...  50.2 us
    reshape x1, local copies, waits for them, and re-layouts, per_device(): integrals.reshape(VBLK, NACT, VBLK, NACT).transpose(0, 2, 1, 3)  26.9 us
    dot_general x1, matrix products, per_device(): lax.dot_general(row_part, flattened, (((0,), (0,)), ((), ())), preferred_...  25.4 us
    transpose x1, local copies, waits for them, and re-layouts, per_device(): reordered = integrals.reshape(VBLK, NACT, VBLK, NACT).transpose(0, 2, 1,...  21.3 us
    unnamed x5, local copies, waits for them, and re-layouts  16.4 us
  transfers between devices with their start and end apart: 2, of which 2 were waited for; matrix products, arithmetic and copies ran while one was open for 3% of the time, Pallas kernels for 0%

commit v1 on v0

v1 whole, which is shorter than its diff:
```python
import functools

import jax
import jax.numpy as jnp
from jax import lax
from jax.experimental import pallas as pl
from jax.experimental.pallas import tpu as pltpu
from jax.sharding import PartitionSpec as P

NACT = 30
VBLK = 48
LANE = 128
HALF = 64
TPAD = 32
WIDTH = VBLK * NACT
WINDOW = -(-(WIDTH + LANE - 32) // LANE) * LANE
UPAIRS = NACT // 2
BF16 = jnp.bfloat16
F32 = jnp.float32


def window_start(block):
    return (block * WIDTH) // LANE * LANE


def gather_body(pairs_ref, in_ref, out_ref):
    out_ref[0] = in_ref[...]


def gather(slabs, pair_blocks):
    rows = slabs.shape[0]
    n = pair_blocks.shape[0]
    return pl.pallas_call(
        gather_body,
        grid_spec=pltpu.PrefetchScalarGridSpec(
            num_scalar_prefetch=1,
            grid=(n, 2),
            in_specs=[
                pl.BlockSpec(
                    (pl.Element(rows), pl.Element(WINDOW)),
                    lambda d, j, pairs: (0, pl.multiple_of(window_start(pairs[d, j]), LANE)),
                )
            ],
            out_specs=pl.BlockSpec((1, rows, WINDOW), lambda d, j, pairs: (d, 0, j)),
        ),
        out_shape=jax.ShapeDtypeStruct((n, rows, 2 * WINDOW), BF16),
        name="gather_blocks",
    )(pair_blocks, slabs)


def exchange_body(n, g_ref, out_ref, recv, acc, local_sem, send_sem, recv_sem):
    me = lax.axis_index("aux")

    barrier = pltpu.get_barrier_semaphore()

    @pl.loop(1, n)
    def _(s):
        pl.semaphore_signal(
            barrier, inc=1, device_id={"aux": lax.rem(me + s, n)}, device_id_type=pl.DeviceIdType.MESH
        )

    own = pltpu.make_async_copy(g_ref.at[me], recv.at[me], local_sem)
    own.start()
    pl.semaphore_wait(barrier, n - 1)

    def send(s):
        to = lax.rem(me + s, n)
        return pltpu.make_async_remote_copy(
            src_ref=g_ref.at[to],
            dst_ref=recv.at[me],
            send_sem=send_sem.at[to],
            recv_sem=recv_sem.at[me],
            device_id={"aux": to},
            device_id_type=pl.DeviceIdType.MESH,
        )

    @pl.loop(1, n)
    def _(s):
        send(s).start()

    acc[...] = jnp.zeros_like(acc)
    own.wait()
    tile = 256

    def add(source):
        @pl.loop(0, WINDOW // tile)
        def _(m):
            at = pl.ds(pl.multiple_of(m * tile, tile), tile)
            acc[at, :] += lax.dot_general(
                recv[source, :, at],
                recv[source, :, WINDOW:],
                (((0,), (0,)), ((), ())),
                preferred_element_type=F32,
            )

    add(me)

    @pl.loop(1, n)
    def _(s):
        source = lax.rem(me + n - s, n)
        pltpu.make_async_remote_copy(
            src_ref=g_ref.at[source],
            dst_ref=recv.at[source],
            send_sem=send_sem.at[source],
            recv_sem=recv_sem.at[source],
            device_id={"aux": source},
            device_id_type=pl.DeviceIdType.MESH,
        ).wait_recv()
        add(source)

    out_ref[...] = acc[...].astype(BF16)

    @pl.loop(1, n)
    def _(s):
        send(s).wait_send()


def exchange(g):
    n, rows, both = g.shape
    return pl.pallas_call(
        functools.partial(exchange_body, n),
        out_shape=jax.ShapeDtypeStruct((WINDOW, WINDOW), BF16),
        in_specs=[pl.BlockSpec(memory_space=pl.ANY)],
        out_specs=pl.BlockSpec(memory_space=pltpu.VMEM),
        scratch_shapes=[
            pltpu.VMEM((n, rows, both), BF16),
            pltpu.VMEM((WINDOW, WINDOW), F32),
            pltpu.SemaphoreType.DMA,
            pltpu.SemaphoreType.DMA((n,)),
            pltpu.SemaphoreType.DMA((n,)),
        ],
        compiler_params=pltpu.CompilerParams(
            collective_id=0, has_side_effects=True, vmem_limit_bytes=56 * 2**20
        ),
        name="exchange_blocks",
    )(g)


def pair_body(i_ref, prow_ref, pcol_ref, r_ref, out_ref, x_ref):
    tile = 256

    @pl.loop(0, VBLK * TPAD // tile)
    def _(m):
        at = pl.ds(pl.multiple_of(m * tile, tile), tile)
        picked = jnp.dot(prow_ref[at, :], i_ref[...], preferred_element_type=F32).astype(BF16)
        x_ref[at, :] = jnp.dot(picked, pcol_ref[...], preferred_element_type=F32).astype(BF16)

    half = UPAIRS * TPAD

    def stacked(a):
        rows = pl.ds(pl.multiple_of(a * TPAD, TPAD), TPAD)
        return jnp.concatenate([x_ref[rows, u * LANE : (u + 1) * LANE] for u in range(UPAIRS)], axis=0)

    low = lax.broadcasted_iota(jnp.int32, (half, LANE), 1) < HALF

    @pl.loop(0, VBLK // 2)
    def _(m):
        first, second = stacked(2 * m), stacked(2 * m + 1)
        x = jnp.concatenate([first, second], axis=1)
        z0 = jnp.dot(r_ref[:, :half], x, preferred_element_type=F32)
        z1 = jnp.dot(r_ref[:, half:], x, preferred_element_type=F32)
        sums = []
        for k, part in enumerate((first, second)):
            lanes = slice(k * LANE, (k + 1) * LANE)
            xf = part.astype(F32)
            turned = pltpu.roll(xf, HALF, 1)
            b0 = jnp.where(low, xf, turned)
            b1 = jnp.where(low, turned, xf)
            t0 = jnp.where(low, z0[:half, lanes], z1[:half, lanes])
            t1 = jnp.where(low, z0[half:, lanes], z1[half:, lanes])
            sums.append(jnp.sum(t0 * b0 + t1 * b1, axis=0, keepdims=True))
        out_ref[m] = jnp.concatenate(sums, axis=0)


def pair_sums(integrals, prow, pcol, r):
    return pl.pallas_call(
        pair_body,
        out_shape=jax.ShapeDtypeStruct((VBLK // 2, 2, LANE), F32),
        in_specs=[pl.BlockSpec(memory_space=pltpu.VMEM)] * 4,
        out_specs=pl.BlockSpec(memory_space=pltpu.VMEM),
        scratch_shapes=[pltpu.VMEM((VBLK * TPAD, UPAIRS * LANE), BF16)],
        compiler_params=pltpu.CompilerParams(vmem_limit_bytes=48 * 2**20),
        name="pair_sums",
    )(integrals, prow, pcol, r)


def selectors(row_block, col_block):
    row_off = row_block * WIDTH - window_start(row_block)
    col_off = col_block * WIDTH - window_start(col_block)
    at = jnp.arange(VBLK * TPAD)
    a, t = at // TPAD, at % TPAD
    want = jnp.where(t < NACT, row_off + a * NACT + t, -1)
    prow = (want[:, None] == jnp.arange(WINDOW)[None, :]).astype(BF16)
    j = jnp.arange(UPAIRS * LANE)
    u, b = 2 * (j // LANE) + (j % LANE) // HALF, j % HALF
    want = jnp.where(b < VBLK, col_off + b * NACT + u, -1)
    pcol = (jnp.arange(WINDOW)[:, None] == want[None, :]).astype(BF16)
    return prow, pcol


def ordered_rdm(rdm):
    half = UPAIRS * TPAD
    j = jnp.arange(2 * half)
    u, t = 2 * ((j % half) // TPAD) + j // half, j % TPAD
    want = jnp.where(t < NACT, t * NACT + u, -1)
    pick = (want[:, None] == jnp.arange(NACT * NACT)[None, :]).astype(BF16)
    once = lax.dot_general(pick, rdm, (((1,), (1,)), ((), ())), preferred_element_type=F32).astype(BF16)
    return lax.dot_general(once, pick, (((1,), (1,)), ((), ())), preferred_element_type=F32).astype(BF16)


def per_device(slabs, rdm, orbital_energy, pair_blocks):
    position = lax.axis_index("aux")
    row_block = pair_blocks[position, 0]
    col_block = pair_blocks[position, 1]
    prow, pcol = selectors(row_block, col_block)
    r = ordered_rdm(rdm)
    integrals = exchange(gather(slabs, pair_blocks))
    raw = pair_sums(integrals, prow, pcol, r)
    paired = raw.reshape(VBLK, 2, HALF).sum(axis=1)[:, :VBLK]
    energy_rows = lax.dynamic_slice_in_dim(orbital_energy, row_block * VBLK, VBLK)
    energy_cols = lax.dynamic_slice_in_dim(orbital_energy, col_block * VBLK, VBLK)
    energy = -paired / (energy_rows[:, None] + energy_cols[None, :])
    weight = jnp.where(row_block == col_block, F32(1.0), F32(2.0))
    total = lax.psum(weight * jnp.sum(energy), "aux")
    mean_energy = total / (VBLK * VBLK * lax.axis_size("aux"))
    return (energy, mean_energy.reshape(1))


def solution(mesh):
    return jax.shard_map(
        per_device,
        mesh=mesh,
        in_specs=(P(("groups", "aux"), None), P("groups", None), P("groups"), P("groups", None)),
        out_specs=(P(("groups", "aux"), None), P("groups")),
        check_vma=False,
    )
```

time: 699 us -> 700 us (level)
  Pallas kernels: 0 us -> 485 us
  waiting for transfers between devices: 395 us -> 0 us
  blocking collectives: 78.8 us -> 187 us
  local copies, waits for them, and re-layouts: 103 us -> 5.28 us
  starting transfers between devices: 57.7 us -> 0 us
  matrix products: 34.2 us -> 5.58 us
  other arithmetic: 21.9 us -> 9.55 us
    pallas_call x0 -> x3, Pallas kernels: none -> 485 us  [the longest x1 414 us: exchange(): pl.pallas_call(functools.partial(exchange_body, n), out_shape=jax.ShapeDt...]
    all_to_all x2 -> x0, waiting for transfers between devices: 395 us -> none  [the longest x1 206 us: per_device(): lax.all_to_all(outgoing_rows, 'aux', split_axis=1, concat_axis=0, tiled=T...]
    psum x1, blocking collectives: 78.8 us -> 187 us  [per_device(): total = lax.psum(weight * jnp.sum(energy), 'aux')]
    all_to_all x2 -> x0, starting transfers between devices: 57.7 us -> none  [the longest x1 50.2 us: per_device(): lax.all_to_all(outgoing_rows, 'aux', split_axis=1, concat_axis=0, tiled=T...]
    reshape x2 -> x1, local copies, waits for them, and re-layouts: 43 us -> 0.11 us  [per_device(): paired = raw.reshape(VBLK, 2, HALF).sum(axis=1)[:, :VBLK]]
    dot_general x2 -> x1, matrix products: 34.2 us -> 5.58 us  [ordered_rdm(): lax.dot_general(once, pick, (((1,), (1,)), ((), ())), preferred_element_t...]
    transpose x1 -> x0, local copies, waits for them, and re-layouts: 21.3 us -> none  [per_device(): reordered = integrals.reshape(VBLK, NACT, VBLK, NACT).transpose(0, 2, 1,...]
    gather x2 -> x0, local copies, waits for them, and re-layouts: 20.9 us -> none  [the longest x1 10.5 us: per_device(): outgoing_cols = jnp.take(blocked, pair_blocks[:, 1], axis=1)]
  transfers between devices with their start and end apart: 2 -> 0, of which waited for: 2 -> 0; matrix products, arithmetic and copies ran while one was open for 3% -> 0% of each run, Pallas kernels for 0% -> 0%
where the time goes in v1:
time: 700 us; the launch traced here: 699 us
  Pallas kernels  485 us (69%)
  blocking collectives  187 us (27%)
  other arithmetic  9.55 us (1%)
    pallas_call x1, Pallas kernels, exchange(): pl.pallas_call(functools.partial(exchange_body, n), out_shape=jax.ShapeDt...  414 us
    psum x1, blocking collectives, per_device(): total = lax.psum(weight * jnp.sum(energy), 'aux')  187 us
    pallas_call x1, Pallas kernels, pair_sums(): pl.pallas_call(pair_body, out_shape=jax.ShapeDtypeStruct((VBLK // 2, 2, L...  40.9 us
    pallas_call x1, Pallas kernels, gather(): pl.pallas_call(gather_body, grid_spec=pltpu.PrefetchScalarGridSpec(num_sc...  30.5 us

profile of v1, /device:TPU:0, one launch (start us, length us, event | category | flops | bytes accessed | tf_op | source)
XLA Modules:
  0.0 699.3 jit_solution(195377389389667670)
XLA Ops:
  0.6 0.0 copy-start
  0.6 1.4 constant_dynamic-slice_fusion.1
  3.3 0.8 fusion.66
  4.1 1.4 copy.6.pairs_ref
  5.5 30.5 %gather_blocks.1.g_ref = bf16[16,250,3072]{2,1,0:T(8,128)(2,1)} custom-call(s32[16,2]{1,0:T(8,128)} %copy.6.pairs_ref, bf16[250,23040]{1,0:T(8,128)(2,1)} %in_ref.1), custom_call_target="tpu_custom_call" | custom-call | tf_op jit(solution)/shard_map/gather_blocks/pallas_call | solution.py:33
  36.0 413.8 %exchange_blocks.1.i_ref = bf16[1536,1536]{1,0:T(8,128)(2,1)} custom-call(bf16[16,250,3072]{2,1,0:T(8,128)(2,1)} %gather_blocks.1.g_ref), custom_call_target="tpu_custom_call" | custom-call | tf_op jit(solution)/shard_map/exchange_blocks/pallas_call | solution.py:120
  450.5 3.0 fusion.1.prow_ref
  454.1 5.1 fusion.pcol_ref
  459.2 0.0 copy-done
  459.2 5.6 fusion.7.r_ref
  464.8 0.0 copy-start.1
  464.8 1.5 copy-done.1
  466.3 40.9 %pair_sums.1 = f32[24,2,128]{2,1,0:T(2,128)S(1)} custom-call(bf16[1536,1536]{1,0:T(8,128)(2,1)} %exchange_blocks.1.i_ref, bf16[1536,1536]{1,0:T(8,128)(2,1)} %fusion.1.prow_ref, bf16[1536,1920]{1,0:T(8,128)(2,1)} %fusion.pcol_ref, bf16[960,960]{1,0:T(8,128)(2,1)S(1)} %copy-done.1), custom_call_target="tpu_custom_call" | custom-call | tf_op jit(solution)/shard_map/pair_sums/pallas_call | solution.py:176
  507.2 0.1 reshape.143
  507.3 0.1 reduce_sum.18
  507.4 1.4 fusion.64
  510.7 186.8 %psum.7 = f32[]{:T(128)} all-reduce(f32[]{:T(128)S(6)} %mul.101), channel_id=1, replica_groups=mesh['groups'=2,'aux'=16] {'aux'}, use_global_device_ids=true, to_apply=%region_2.3 | all-reduce | flops 1 | bytes 8 | tf_op jit(solution)/shard_map/psum | solution.py:224
  (3 shorter events, 0.0 us)
Async XLA Ops:
  0.6 458.6 %copy-start = (bf16[900,900]{1,0:T(8,128)(2,1)S(1)}, bf16[900,900]{1,0:T(8,128)(2,1)}, u32[]{:S(2)}) copy-start(bf16[900,900]{1,0:T(8,128)(2,1)} %param.5) | copy-start | bytes 4860004
  464.8 1.5 copy-start.1

commit v2 on v1

--- a/solution.py
+++ b/solution.py
@@ -48,33 +48,38 @@
     )(pair_blocks, slabs)
 
 
-def exchange_body(n, g_ref, out_ref, recv, acc, local_sem, send_sem, recv_sem):
-    me = lax.axis_index("aux")
+def exchange_body(size, g_ref, shift_ref, out_ref, recv, acc, local_sem, send_sem, recv_sem):
+    position = lax.axis_index("aux")
+    base = position // size * size
+    me = position - base
+
+    def device(member):
+        return {"aux": base + member}
 
     barrier = pltpu.get_barrier_semaphore()
 
-    @pl.loop(1, n)
+    @pl.loop(1, size)
     def _(s):
         pl.semaphore_signal(
-            barrier, inc=1, device_id={"aux": lax.rem(me + s, n)}, device_id_type=pl.DeviceIdType.MESH
+            barrier, inc=1, device_id=device(lax.rem(me + s, size)), device_id_type=pl.DeviceIdType.MESH
         )
 
     own = pltpu.make_async_copy(g_ref.at[me], recv.at[me], local_sem)
     own.start()
-    pl.semaphore_wait(barrier, n - 1)
+    pl.semaphore_wait(barrier, size - 1)
 
     def send(s):
-        to = lax.rem(me + s, n)
+        to = lax.rem(me + s, size)
         return pltpu.make_async_remote_copy(
             src_ref=g_ref.at[to],
             dst_ref=recv.at[me],
             send_sem=send_sem.at[to],
             recv_sem=recv_sem.at[me],
-            device_id={"aux": to},
+            device_id=device(to),
             device_id_type=pl.DeviceIdType.MESH,
         )
 
-    @pl.loop(1, n)
+    @pl.loop(1, size)
     def _(s):
         send(s).start()
 
@@ -95,45 +100,58 @@
 
     add(me)
 
-    @pl.loop(1, n)
-    def _(s):
-        source = lax.rem(me + n - s, n)
+    @pl.loop(1, size)
+    def _(s):
+        source = lax.rem(me + size - s, size)
         pltpu.make_async_remote_copy(
             src_ref=g_ref.at[source],
             dst_ref=recv.at[source],
             send_sem=send_sem.at[source],
             recv_sem=recv_sem.at[source],
-            device_id={"aux": source},
+            device_id=device(source),
             device_id_type=pl.DeviceIdType.MESH,
         ).wait_recv()
         add(source)
 
-    out_ref[...] = acc[...].astype(BF16)
-
-    @pl.loop(1, n)
+    shift = shift_ref[0]
+    piece = 96
+
+    @pl.loop(0, WIDTH // piece)
+    def _(m):
+        def from_row(offset):
+            return acc[pl.ds(pl.multiple_of(m * piece + offset, 32), piece), :]
+
+        low = jnp.where(shift == 0, from_row(0), from_row(32))
+        high = jnp.where(shift == 64, from_row(64), from_row(96))
+        out_ref[pl.ds(pl.multiple_of(m * piece, 32), piece), :] = jnp.where(shift < 64, low, high)
+
+    @pl.loop(1, size)
     def _(s):
         send(s).wait_send()
 
 
-def exchange(g):
-    n, rows, both = g.shape
+def exchange(g, shift, identity):
+    size, rows, both = g.shape
     return pl.pallas_call(
-        functools.partial(exchange_body, n),
-        out_shape=jax.ShapeDtypeStruct((WINDOW, WINDOW), BF16),
-        in_specs=[pl.BlockSpec(memory_space=pl.ANY)],
+        functools.partial(exchange_body, size),
+        out_shape=jax.ShapeDtypeStruct((WIDTH, WINDOW), F32),
+        in_specs=[pl.BlockSpec(memory_space=pl.ANY), pl.BlockSpec(memory_space=pltpu.SMEM)],
         out_specs=pl.BlockSpec(memory_space=pltpu.VMEM),
         scratch_shapes=[
-            pltpu.VMEM((n, rows, both), BF16),
+            pltpu.VMEM((size, rows, both), BF16),
             pltpu.VMEM((WINDOW, WINDOW), F32),
             pltpu.SemaphoreType.DMA,
-            pltpu.SemaphoreType.DMA((n,)),
-            pltpu.SemaphoreType.DMA((n,)),
+            pltpu.SemaphoreType.DMA((size,)),
+            pltpu.SemaphoreType.DMA((size,)),
         ],
         compiler_params=pltpu.CompilerParams(
-            collective_id=0, has_side_effects=True, vmem_limit_bytes=56 * 2**20
+            collective_id=identity, has_side_effects=True, vmem_limit_bytes=40 * 2**20
         ),
-        name="exchange_blocks",
-    )(g)
+        cost_estimate=pl.CostEstimate(
+            flops=200 * size * rows * WINDOW * WINDOW, bytes_accessed=2 * size * rows * both, transcendentals=0
+        ),
+        name=f"exchange_blocks_{identity}",
+    )(g, shift)
 
 
 def pair_body(i_ref, prow_ref, pcol_ref, r_ref, out_ref, x_ref):
@@ -184,13 +202,12 @@
     )(integrals, prow, pcol, r)
 
 
-def selectors(row_block, col_block):
-    row_off = row_block * WIDTH - window_start(row_block)
+def selectors(col_block):
     col_off = col_block * WIDTH - window_start(col_block)
     at = jnp.arange(VBLK * TPAD)
     a, t = at // TPAD, at % TPAD
-    want = jnp.where(t < NACT, row_off + a * NACT + t, -1)
-    prow = (want[:, None] == jnp.arange(WINDOW)[None, :]).astype(BF16)
+    want = jnp.where(t < NACT, a * NACT + t, -1)
+    prow = (want[:, None] == jnp.arange(WIDTH)[None, :]).astype(BF16)
     j = jnp.arange(UPAIRS * LANE)
     u, b = 2 * (j // LANE) + (j % LANE) // HALF, j % HALF
     want = jnp.where(b < VBLK, col_off + b * NACT + u, -1)
@@ -212,9 +229,25 @@
     position = lax.axis_index("aux")
     row_block = pair_blocks[position, 0]
     col_block = pair_blocks[position, 1]
-    prow, pcol = selectors(row_block, col_block)
+    prow, pcol = selectors(col_block)
     r = ordered_rdm(rdm)
-    integrals = exchange(gather(slabs, pair_blocks))
+    count = lax.axis_size("aux")
+    size = count // 2
+    half = position // size
+    mine = lax.dynamic_slice_in_dim(pair_blocks, half * size, size)
+    others = lax.dynamic_slice_in_dim(pair_blocks, (1 - half) * size, size)
+    partner_row = others[position % size, 0]
+
+    def shift(block):
+        return (block * WIDTH - window_start(block)).reshape(1)
+
+    theirs = exchange(gather(slabs, others), shift(partner_row), 0)
+    top = jnp.maximum(jnp.max(jnp.abs(theirs)), F32(1e-30))
+    swap = [(i, (i + size) % count) for i in range(count)]
+    coded = lax.ppermute((theirs * (1 / top)).astype(jnp.float16), "aux", swap)
+    their_top = lax.ppermute(top.reshape(1), "aux", swap)
+    kept = exchange(gather(slabs, mine), shift(row_block), 1)
+    integrals = (kept + coded.astype(F32) * their_top).astype(BF16)
     raw = pair_sums(integrals, prow, pcol, r)
     paired = raw.reshape(VBLK, 2, HALF).sum(axis=1)[:, :VBLK]
     energy_rows = lax.dynamic_slice_in_dim(orbital_energy, row_block * VBLK, VBLK)

time: 700 us -> 640 us (0.914)
  blocking collectives: 187 us -> 43.3 us
  starting transfers between devices: 0 us -> 92.9 us
  Pallas kernels: 485 us -> 450 us
  other arithmetic: 9.55 us -> 26.9 us
    psum x1, blocking collectives: 187 us -> 43.3 us  [per_device(): total = lax.psum(weight * jnp.sum(energy), 'aux')]
    ppermute x0 -> x2, starting transfers between devices: none -> 92.9 us  [the longest x1 90.1 us: per_device(): their_top = lax.ppermute(top.reshape(1), 'aux', swap)]
    pallas_call x1 -> x2, Pallas kernels: 414 us -> 377 us  [exchange(): pl.pallas_call(functools.partial(exchange_body, size), out_shape=jax.Shap...]
    convert_element_type x1 -> x3, other arithmetic: 3 us -> 19 us  [the longest x1 9.2 us: per_device(): integrals = (kept + coded.astype(F32) * their_top).astype(BF16)]
    pallas_call x1 -> x2, Pallas kernels: 30.5 us -> 32.2 us  [gather(): pl.pallas_call(gather_body, grid_spec=pltpu.PrefetchScalarGridSpec(num_sc...]
  transfers between devices with their start and end apart: 0 -> 2, of which waited for: 0 -> 0; matrix products, arithmetic and copies ran while one was open for 0% -> 2% of each run, Pallas kernels for 0% -> 40%
where the time goes in v2:
time: 640 us; the launch traced here: 639 us
  Pallas kernels  450 us (70%)
  starting transfers between devices  92.9 us (15%)
  blocking collectives  43.3 us (7%)
  other arithmetic  26.9 us (4%)
  local copies, waits for them, and re-layouts  12 us (2%)
  between operations  8.45 us (1%)
    pallas_call x2, Pallas kernels, exchange(): pl.pallas_call(functools.partial(exchange_body, size), out_shape=jax.Shap...  377 us
    ppermute x1, starting transfers between devices, per_device(): their_top = lax.ppermute(top.reshape(1), 'aux', swap)  90.1 us
    psum x1, blocking collectives, per_device(): total = lax.psum(weight * jnp.sum(energy), 'aux')  43.3 us
    pallas_call x1, Pallas kernels, pair_sums(): pl.pallas_call(pair_body, out_shape=jax.ShapeDtypeStruct((VBLK // 2, 2, L...  40.8 us
    pallas_call x2, Pallas kernels, gather(): pl.pallas_call(gather_body, grid_spec=pltpu.PrefetchScalarGridSpec(num_sc...  32.2 us
  transfers between devices with their start and end apart: 2, of which 0 were waited for; matrix products, arithmetic and copies ran while one was open for 2% of the time, Pallas kernels for 40%

profile of v2, /device:TPU:0, one launch (start us, length us, event | category | flops | bytes accessed | tf_op | source)
XLA Modules:
  0.0 639.0 jit_solution(10768488337044722286)
XLA Ops:
  0.7 1.5 constant_dynamic-slice_fusion
  2.8 1.4 constant_dynamic-slice_fusion.1
  4.2 0.7 copy.9.pairs_ref
  4.9 16.0 %gather_blocks.3.g_ref = bf16[8,250,3072]{2,1,0:T(8,128)(2,1)} custom-call(s32[8,2]{1,0:T(8,128)} %copy.9.pairs_ref, bf16[250,23040]{1,0:T(8,128)(2,1)} %in_ref.3), custom_call_target="tpu_custom_call" | custom-call | tf_op jit(solution)/shard_map/gather_blocks/pallas_call | solution.py:33
  20.9 139.8 %exchange_blocks_0.1 = f32[1440,1536]{1,0:T(8,128)S(1)} custom-call(bf16[8,250,3072]{2,1,0:T(8,128)(2,1)} %gather_blocks.3.g_ref, s32[1]{0:T(128)} %bitcast.3.shift_ref), custom_call_target="tpu_custom_call" | custom-call | flops 943718400000 | bytes 12288000 | tf_op jit(solution)/shard_map/exchange_blocks_0/pallas_call | solution.py:135
  160.8 3.4 copy-done.1
  164.2 1.4 abs_reduce_fusion
  166.2 6.8 %multiply_convert_fusion = f16[1440,1536]{1,0:T(8,128)(2,1)} fusion(f32[1440,1536]{1,0:T(8,128)} %copy-done.1, f32[]{:T(128)S(6)} %div.101), kind=kLoop, calls=%fused_computation.5 | loop fusion | flops 4423680 | bytes 13271044 | tf_op jit(solution)/shard_map/convert_element_type | solution.py:247
  173.1 2.8 collective-permute-start
  175.8 90.1 %collective-permute-start.1 = (f32[1]{0:T(128)}, f32[1]{0:T(128)}, u32[]{:S(2)}, u32[]{:S(2)}) collective-permute-start(f32[1]{0:T(128)} %bitcast.4), channel_id=1, source_target_pairs={{0,8},{1,9},{2,10},{3,11},{4,12},{5,13},{6,14},{7,15},{8,0},{9,1},... | collective-permute-start | bytes 20 | tf_op jit(solution)/shard_map/ppermute | solution.py:248
  266.7 0.7 copy.8.pairs_ref
  267.3 16.2 %gather_blocks.2.g_ref = bf16[8,250,3072]{2,1,0:T(8,128)(2,1)} custom-call(s32[8,2]{1,0:T(8,128)} %copy.8.pairs_ref, bf16[250,23040]{1,0:T(8,128)(2,1)} %in_ref.3), custom_call_target="tpu_custom_call" | custom-call | tf_op jit(solution)/shard_map/gather_blocks/pallas_call | solution.py:33
  283.5 237.0 %exchange_blocks_1.1 = f32[1440,1536]{1,0:T(8,128)S(1)} custom-call(bf16[8,250,3072]{2,1,0:T(8,128)(2,1)} %gather_blocks.2.g_ref, s32[1]{0:T(128)} %bitcast.1.shift_ref), custom_call_target="tpu_custom_call" | custom-call | flops 943718400000 | bytes 12288000 | tf_op jit(solution)/shard_map/exchange_blocks_1/pallas_call | solution.py:135
  520.5 3.4 copy-done.2
  527.1 0.8 fusion.67
  528.0 5.7 fusion.7.r_ref
  533.7 5.1 fusion.pcol_ref
  538.9 3.0 fusion.1.prow_ref
  541.8 9.2 %add_convert_fusion.i_ref = bf16[1440,1536]{1,0:T(8,128)(2,1)} fusion(f32[1440,1536]{1,0:T(8,128)} %copy-done.2, f16[1440,1536]{1,0:T(8,128)(2,1)} %collective-permute-done, f32[]{:T(128)} %bitcast.5), kind=kLoop, calls=%fused_computation.4 | loop fusion | flops 8847360 | bytes 17694724 | tf_op jit(solution)/shard_map/convert_element_type | solution.py:250
  551.0 40.8 %pair_sums.1 = f32[24,2,128]{2,1,0:T(2,128)S(1)} custom-call(bf16[1440,1536]{1,0:T(8,128)(2,1)} %add_convert_fusion.i_ref, bf16[1536,1440]{1,0:T(8,128)(2,1)} %fusion.1.prow_ref, bf16[1536,1920]{1,0:T(8,128)(2,1)} %fusion.pcol_ref, bf16[960,960]{1,0:T(8,128)(2,1)S(1)} %copy-done.3), custom_call_target="tpu_custom_call" | custom-call | tf_op jit(solution)/shard_map/pair_sums/pallas_call | solution.py:194
  591.9 0.1 reshape.157
  592.0 0.1 reduce_sum.18
  592.0 1.3 fusion.65
  594.0 43.3 %psum.7 = f32[]{:T(128)} all-reduce(f32[]{:T(128)S(6)} %mul.143), channel_id=1, replica_groups=mesh['groups'=2,'aux'=16] {'aux'}, use_global_device_ids=true, to_apply=%region_3.4 | all-reduce | flops 1 | bytes 8 | tf_op jit(solution)/shard_map/psum | solution.py:257
  (13 shorter events, 0.1 us)
Async XLA Ops:
  0.6 527.4 %copy-start = (bf16[900,900]{1,0:T(8,128)(2,1)S(1)}, bf16[900,900]{1,0:T(8,128)(2,1)}, u32[]{:S(2)}) copy-start(bf16[900,900]{1,0:T(8,128)(2,1)} %param.5) | copy-start | bytes 4860004
  160.8 3.4 copy-start.1
  166.2 100.4 %copy-start.4 = (s32[8,2]{0,1:T(2,128)S(1)}, s32[8,2]{0,1:T(2,128)}, u32[]{:S(2)}) copy-start(s32[8,2]{0,1:T(2,128)} %get-tuple-element.10) | copy-start | bytes 196
  173.1 368.7 %collective-permute-start = (f16[1440,1536]{1,0:T(8,128)(2,1)}, f16[1440,1536]{1,0:T(8,128)(2,1)}, u32[]{:S(2)}, u32[]{:S(2)}) collective-permute-start(f16[1440,1536]{1,0:T(8,128)(2,1)} %multiply_convert_fusion), channel_id=1, source_target_pairs={{0,8},{1,9},{2,10},{3,11},{4,12},{5,13},{6,14},{7,15},{8,0},{9,1},... | collective-permute-start | bytes 13271048 | tf_op jit(solution)/shard_map/ppermute | solution.py:247
  175.8 366.0 %collective-permute-start.1 = (f32[1]{0:T(128)}, f32[1]{0:T(128)}, u32[]{:S(2)}, u32[]{:S(2)}) collective-permute-start(f32[1]{0:T(128)} %bitcast.4), channel_id=1, source_target_pairs={{0,8},{1,9},{2,10},{3,11},{4,12},{5,13},{6,14},{7,15},{8,0},{9,1},... | collective-permute-start | bytes 20 | tf_op jit(solution)/shard_map/ppermute | solution.py:248
  520.5 3.4 copy-start.2
  541.8 9.2 %copy-start.3 = (bf16[960,960]{1,0:T(8,128)(2,1)S(1)}, bf16[960,960]{1,0:T(8,128)(2,1)}, u32[]{:S(2)}) copy-start(bf16[960,960]{1,0:T(8,128)(2,1)} %fusion.7.r_ref) | copy-start | bytes 5529604

commit v3 on v2

--- a/solution.py
+++ b/solution.py
@@ -244,8 +244,9 @@
     theirs = exchange(gather(slabs, others), shift(partner_row), 0)
     top = jnp.maximum(jnp.max(jnp.abs(theirs)), F32(1e-30))
     swap = [(i, (i + size) % count) for i in range(count)]
+    their_top = lax.ppermute(top.reshape(1), "aux", swap)
+    theirs, top, their_top = lax.optimization_barrier((theirs, top, their_top))
     coded = lax.ppermute((theirs * (1 / top)).astype(jnp.float16), "aux", swap)
-    their_top = lax.ppermute(top.reshape(1), "aux", swap)
     kept = exchange(gather(slabs, mine), shift(row_block), 1)
     integrals = (kept + coded.astype(F32) * their_top).astype(BF16)
     raw = pair_sums(integrals, prow, pcol, r)

time: 640 us -> 557 us (0.87)
  starting transfers between devices: 92.9 us -> 4.29 us
  blocking collectives: 43.3 us -> 59.8 us
  Pallas kernels: 450 us -> 439 us
    ppermute x1, starting transfers between devices: 90.1 us -> 3.95 us  [per_device(): their_top = lax.ppermute(top.reshape(1), 'aux', swap)]
    psum x1, blocking collectives: 43.3 us -> 59.8 us  [per_device(): total = lax.psum(weight * jnp.sum(energy), 'aux')]
    pallas_call x2, Pallas kernels: 377 us -> 366 us  [exchange(): pl.pallas_call(functools.partial(exchange_body, size), out_shape=jax.Shap...]
  transfers between devices with their start and end apart: 2 -> 2, of which waited for: 0 -> 0; matrix products, arithmetic and copies ran while one was open for 2% -> 3% of each run, Pallas kernels for 40% -> 44%
where the time goes in v3:
time: 557 us; the launch traced here: 556 us
  Pallas kernels  439 us (79%)
  blocking collectives  59.8 us (11%)
  other arithmetic  26.8 us (5%)
  local copies, waits for them, and re-layouts  11.9 us (2%)
  between operations  8.45 us (2%)
  matrix products  5.72 us (1%)
    pallas_call x2, Pallas kernels, exchange(): pl.pallas_call(functools.partial(exchange_body, size), out_shape=jax.Shap...  366 us
    psum x1, blocking collectives, per_device(): total = lax.psum(weight * jnp.sum(energy), 'aux')  59.8 us
    pallas_call x1, Pallas kernels, pair_sums(): pl.pallas_call(pair_body, out_shape=jax.ShapeDtypeStruct((VBLK // 2, 2, L...  40.8 us
    pallas_call x2, Pallas kernels, gather(): pl.pallas_call(gather_body, grid_spec=pltpu.PrefetchScalarGridSpec(num_sc...  32 us
  transfers between devices with their start and end apart: 2, of which 0 were waited for; matrix products, arithmetic and copies ran while one was open for 3% of the time, Pallas kernels for 44%

profile of v3, /device:TPU:0, one launch (start us, length us, event | category | flops | bytes accessed | tf_op | source)
XLA Modules:
  0.0 555.6 jit_solution(12523892315569778160)
XLA Ops:
  0.7 1.5 constant_dynamic-slice_fusion
  2.8 1.4 constant_dynamic-slice_fusion.1
  4.2 0.7 copy.9.pairs_ref
  4.9 16.0 %gather_blocks.3.g_ref = bf16[8,250,3072]{2,1,0:T(8,128)(2,1)} custom-call(s32[8,2]{1,0:T(8,128)} %copy.9.pairs_ref, bf16[250,23040]{1,0:T(8,128)(2,1)} %in_ref.3), custom_call_target="tpu_custom_call" | custom-call | tf_op jit(solution)/shard_map/gather_blocks/pallas_call | solution.py:33
  20.9 139.8 %exchange_blocks_0.1 = f32[1440,1536]{1,0:T(8,128)S(1)} custom-call(bf16[8,250,3072]{2,1,0:T(8,128)(2,1)} %gather_blocks.3.g_ref, s32[1]{0:T(128)} %bitcast.3.shift_ref), custom_call_target="tpu_custom_call" | custom-call | flops 943718400000 | bytes 12288000 | tf_op jit(solution)/shard_map/exchange_blocks_0/pallas_call | solution.py:135
  160.7 3.3 copy-done.1
  164.0 1.4 abs_reduce_fusion
  166.1 4.0 collective-permute-start
  170.7 0.7 copy.8.pairs_ref
  171.4 16.0 %gather_blocks.2.g_ref = bf16[8,250,3072]{2,1,0:T(8,128)(2,1)} custom-call(s32[8,2]{1,0:T(8,128)} %copy.8.pairs_ref, bf16[250,23040]{1,0:T(8,128)(2,1)} %in_ref.3), custom_call_target="tpu_custom_call" | custom-call | tf_op jit(solution)/shard_map/gather_blocks/pallas_call | solution.py:33
  187.5 6.8 %multiply_convert_fusion = f16[1440,1536]{1,0:T(8,128)(2,1)} fusion(f32[1440,1536]{1,0:T(8,128)} %copy-done.1, f32[]{:T(128)S(6)} %div.101), kind=kLoop, calls=%fused_computation.5 | loop fusion | flops 4423680 | bytes 13271044 | tf_op jit(solution)/shard_map/convert_element_type | solution.py:249
  194.3 0.3 collective-permute-start.1
  194.7 226.0 %exchange_blocks_1.1 = f32[1440,1536]{1,0:T(8,128)S(1)} custom-call(bf16[8,250,3072]{2,1,0:T(8,128)(2,1)} %gather_blocks.2.g_ref, s32[1]{0:T(128)} %bitcast.1.shift_ref), custom_call_target="tpu_custom_call" | custom-call | flops 943718400000 | bytes 12288000 | tf_op jit(solution)/shard_map/exchange_blocks_1/pallas_call | solution.py:135
  420.6 3.4 copy-done.2
  427.2 0.8 fusion.67
  428.1 5.7 %fusion.7.r_ref = bf16[960,960]{1,0:T(8,128)(2,1)} fusion(s32[960]{0:T(1024)S(1)} %fusion.54, bf16[900,900]{1,0:T(8,128)(2,1)S(1)} %copy-done), kind=kOutput, calls=%fused_computation.13 | convolution fusion | flops 3217593600 | bytes 3467040 | tf_op jit(solution)/shard_map/dot_general | solution.py:225
  433.9 5.1 fusion.pcol_ref
  439.0 3.0 fusion.1.prow_ref
  442.0 9.1 %add_convert_fusion.i_ref = bf16[1440,1536]{1,0:T(8,128)(2,1)} fusion(f32[1440,1536]{1,0:T(8,128)} %copy-done.2, f16[1440,1536]{1,0:T(8,128)(2,1)} %collective-permute-done.1, f32[]{:T(128)} %bitcast.5), kind=kLoop, calls=%fused_computation.4 | loop fusion | flops 8847360 | bytes 17694724 | tf_op jit(solution)/shard_map/convert_element_type | solution.py:251
  451.1 40.8 %pair_sums.1 = f32[24,2,128]{2,1,0:T(2,128)S(1)} custom-call(bf16[1440,1536]{1,0:T(8,128)(2,1)} %add_convert_fusion.i_ref, bf16[1536,1440]{1,0:T(8,128)(2,1)} %fusion.1.prow_ref, bf16[1536,1920]{1,0:T(8,128)(2,1)} %fusion.pcol_ref, bf16[960,960]{1,0:T(8,128)(2,1)S(1)} %copy-done.3), custom_call_target="tpu_custom_call" | custom-call | tf_op jit(solution)/shard_map/pair_sums/pallas_call | solution.py:194
  491.9 0.1 reshape.157
  492.0 0.1 reduce_sum.18
  492.1 1.3 fusion.65
  494.0 59.8 %psum.7 = f32[]{:T(128)} all-reduce(f32[]{:T(128)S(6)} %mul.143), channel_id=1, replica_groups=mesh['groups'=2,'aux'=16] {'aux'}, use_global_device_ids=true, to_apply=%region_3.4 | all-reduce | flops 1 | bytes 8 | tf_op jit(solution)/shard_map/psum | solution.py:258
  (13 shorter events, 0.1 us)
Async XLA Ops:
  0.6 427.5 %copy-start = (bf16[900,900]{1,0:T(8,128)(2,1)S(1)}, bf16[900,900]{1,0:T(8,128)(2,1)}, u32[]{:S(2)}) copy-start(bf16[900,900]{1,0:T(8,128)(2,1)} %param.5) | copy-start | bytes 4860004
  160.7 3.3 copy-start.1
  164.0 6.7 %copy-start.4 = (s32[8,2]{0,1:T(2,128)S(1)}, s32[8,2]{0,1:T(2,128)}, u32[]{:S(2)}) copy-start(s32[8,2]{0,1:T(2,128)} %get-tuple-element.16) | copy-start | bytes 196
  166.1 21.3 %collective-permute-start = (f32[1]{0:T(128)}, f32[1]{0:T(128)}, u32[]{:S(2)}, u32[]{:S(2)}) collective-permute-start(f32[1]{0:T(128)} %bitcast.4), channel_id=1, source_target_pairs={{0,8},{1,9},{2,10},{3,11},{4,12},{5,13},{6,14},{7,15},{8,0},{9,1},... | collective-permute-start | bytes 20 | tf_op jit(solution)/shard_map/ppermute | solution.py:247
  194.3 247.6 %collective-permute-start.1 = (f16[1440,1536]{1,0:T(8,128)(2,1)}, f16[1440,1536]{1,0:T(8,128)(2,1)}, u32[]{:S(2)}, u32[]{:S(2)}) collective-permute-start(f16[1440,1536]{1,0:T(8,128)(2,1)} %multiply_convert_fusion), channel_id=1, source_target_pairs={{0,8},{1,9},{2,10},{3,11},{4,12},{5,13},{6,14},{7,15},{8,0},{9,1},... | collective-permute-start | bytes 13271048 | tf_op jit(solution)/shard_map/ppermute | solution.py:249
  420.6 3.4 copy-start.2
  442.0 9.1 %copy-start.3 = (bf16[960,960]{1,0:T(8,128)(2,1)S(1)}, bf16[960,960]{1,0:T(8,128)(2,1)}, u32[]{:S(2)}) copy-start(bf16[960,960]{1,0:T(8,128)(2,1)} %fusion.7.r_ref) | copy-start | bytes 5529604
